TPU v7x, 32 devices: a whole 2x2x4 slice. The times are simulated.
32 devices in a mesh: gx: 8 (over y, x, core), gy: 4 (over z).
Axes of the slice: x: 2, y: 2, z: 4, core: 2. Of those that a mesh axis runs over, the one named last changes fastest.
Arguments:
- probes: float32 [16, 128, 128, 256], P(None, 'gx', 'gy'), may hold values from -6 to 6
- diffusivity: float32 [128, 128, 256], P('gx', 'gy'), may hold values from 0.5 to 2
- wind_speed: float32 [3], replicated, may hold values from 0.5 to 2
- sensor_cell: int32 [8, 4, 128], P('gx', 'gy'), may hold values from 0 to 131071
- sensor_owner: int32 [8, 4, 128, 1], P('gx', 'gy'), may hold values from 0 to 31; in each aligned block of 128 rows (0 to 127, 128 to 255, ..., all dimensions but the last counted through in order) at most 4 rows name the same one
- sensor_count: int32 [8, 4], P('gx', 'gy'), may hold values from 64 to 128
- goal_weight: float32 [8, 4, 128, 16], P('gx', 'gy'), may hold values from -0.6 to 0.6
Outputs:
- fields: float32 [16, 128, 128, 256], P(None, 'gx', 'gy')
- goal_block: float32 [512, 16], P(('gx', 'gy'))
- ritz_gram: float32 [16, 16], replicated
Inputs may be any that keep to these rules, and one draw needn't show every extreme that they name: `sensor_owner`: among the rows of one device, no owner is named more than 4 times, a bound that some block reaches.
All inputs are finite; a program needn't handle non-finite values.
Results may differ from a plain program's by a relative error of at most 0.0003.
Values sent between devices are 32-bit elements; how exact they have to be, the bound alone decides.
A program may use at most 192 MiB of HBM per device.

v0:
```python
import jax
import jax.numpy as jnp
from jax import lax
from jax.sharding import PartitionSpec as P

STEPS = 2
SWEEPS = 4
time_step = 2.0


def padded_2(cells, sides, width):
    for axis, dim in sides:
        count = lax.axis_size(axis)
        ends = count - 1
        head = lax.slice_in_dim(cells, 0, width, axis=dim)
        tail = lax.slice_in_dim(cells, cells.shape[dim] - width, cells.shape[dim], axis=dim)
        cells = jnp.concatenate(
            [
                lax.ppermute(tail, axis, [(i, (i + 1) % count) for i in range(ends)]),
                cells,
                lax.ppermute(head, axis, [((i + 1) % count, i) for i in range(ends)]),
            ],
            axis=dim,
        )
    return cells


def relax(padded, source, diffusion, wind_speed):
    centre = padded[..., 1:-1, 1:-1, :]
    widths = [(0, 0)] * (centre.ndim - 1) + [(1, 1)]
    zpadded = jnp.pad(centre, widths)
    beside = padded[..., 2:, 1:-1, :] + padded[..., :-2, 1:-1, :]
    beside = beside + padded[..., 1:-1, 2:, :] + padded[..., 1:-1, :-2, :]
    beside = beside + zpadded[..., 2:] + zpadded[..., :-2]
    upwind = (
        wind_speed[0] * padded[..., :-2, 1:-1, :]
        + wind_speed[1] * padded[..., 1:-1, :-2, :]
        + wind_speed[2] * zpadded[..., :-2]
    )
    diagonal = 1.0 + time_step * (6.0 * diffusion + wind_speed[0] + wind_speed[1] + wind_speed[2])
    updated = (source + time_step * (diffusion * beside + upwind)) / diagonal
    return jnp.where(diffusion > 0.0, updated, 0.0)


def body(probes, diffusivity, wind_speed, sensor_cell, sensor_owner, sensor_count, goal_weight):
    state_field = probes
    for step_index in range(STEPS):
        source = state_field
        for sweep_index in range(SWEEPS):
            padded = padded_2(state_field, (("gx", 1), ("gy", 2)), 1)
            state_field = relax(padded, source, diffusivity, wind_speed)
    probe_count = state_field.shape[0]
    sensor_rows = sensor_cell.shape[2]
    goal_count = goal_weight.shape[3]
    device_count = lax.axis_size("gx") * lax.axis_size("gy")
    capacity = max(2, (sensor_rows + device_count - 1) // device_count)
    flattened = state_field.reshape(probe_count, -1)
    readings = jnp.take(flattened, sensor_cell.reshape(-1), axis=1)
    row_index = jnp.arange(sensor_rows, dtype=jnp.int32)
    active = (row_index < sensor_count.reshape(())).astype(jnp.float32)
    readings = readings.T * active[:, None]
    weights = goal_weight.reshape(sensor_rows, goal_count)
    owners = sensor_owner.reshape(sensor_rows)
    earlier = (owners[None, :] == owners[:, None]) & (row_index[None, :] < row_index[:, None])
    slot_rank = jnp.sum(earlier.astype(jnp.int32), axis=1)
    slot_index = owners * capacity + slot_rank
    placing = (
        jnp.arange(device_count * capacity, dtype=jnp.int32)[:, None] == slot_index[None, :]
    ).astype(jnp.float32)
    payload = jnp.concatenate([readings, weights], axis=1)
    outgoing = jnp.dot(placing, payload, precision=lax.Precision.HIGHEST).reshape(
        device_count, capacity, probe_count + goal_count
    )
    received = lax.all_to_all(outgoing, ("gx", "gy"), split_axis=0, concat_axis=0, tiled=True)
    goal_block = jnp.einsum(
        "scj,scp->jp",
        received[..., probe_count:],
        received[..., :probe_count],
        precision=lax.Precision.HIGHEST,
    )
    ritz_gram = lax.psum(
        jnp.dot(goal_block.T, goal_block, precision=lax.Precision.HIGHEST), ("gx", "gy")
    )
    return (state_field, goal_block, ritz_gram)


def solution(mesh):
    placed = (
        P(None, "gx", "gy", None),
        P("gx", "gy", None),
        P(),
        P("gx", "gy", None),
        P("gx", "gy", None, None),
        P("gx", "gy"),
        P("gx", "gy", None, None),
    )
    return jax.shard_map(
        body,
        mesh=mesh,
        in_specs=placed,
        out_specs=(P(None, "gx", "gy", None), P(("gx", "gy"), None), P()),
        check_vma=False,
    )
```

profile of v0, /device:TPU:0, one launch (start us, length us, event | category | flops | bytes accessed | tf_op | source)
XLA Modules:
  0.0 530.0 jit_solution(1779432885856855623)
XLA Ops:
  0.7 10.1 %copy.60 = f32[16,16,32,256]{3,0,2,1:T(8,128)S(1)} copy(f32[16,16,32,256]{3,2,1,0:T(8,128)} %param.7) | data formatting | bytes 16777216 | tf_op args[0]
  10.8 2.4 collective-permute-start.1
  13.3 1.8 collective-permute-start
  16.0 10.0 %constant_dynamic-update-slice_fusion.1 = f32[16,18,32,256]{3,0,2,1:T(8,128)} fusion(f32[16,18,32,256]{3,0,2,1:T(8,128)} %constant_dynamic-update-slice_fusion.2, f32[16,16,32,256]{3,2,1,0:T(8,128)S(1)} %copy-done), kind=kLoop, calls=%fused_computation.202 | loop fusion | bytes 16777216
  29.3 4.9 collective-permute-start.3
  34.9 2.1 multiply_add_fusion
  38.4 25.3 %fusion.81 = f32[16,16,32,256]{3,0,2,1:T(8,128)} fusion(f32[16,16,32,256]{3,0,2,1:T(8,128)} %copy-done.2, f32[16,18,32,256]{3,0,2,1:T(8,128)} %constant_dynamic-update-slice_fusion, f32[16,18,1,256]{3,0,2,1:T(8,128)S(1)} %collective-permute-done.3, f32[16,18,1,256]{3,0,2,1:T(8,128)S(1)} %collective-permute-done.2, ...), kind=kLoop, calls=%fused_computation.158 | loop fusion | flops 41943040 | bytes 29032460 | tf_op jit(solution)/shard_map/jit(_where)/select_n | solution.py:42
  66.3 7.8 %collective-permute-start.5 = (f32[16,1,32,256]{3,0,2,1:T(8,128)S(1)}, f32[16,1,32,256]{3,0,2,1:T(8,128)S(1)}, u32[]{:S(2)}, u32[]{:S(2)}) collective-permute-start(f32[16,1,32,256]{3,0,2,1:T(8,128)S(1)} %get-tuple-element.40), channel_id=1, source_target_pairs={{0,4},{4,8},{8,12},{12,16},{16,20},{20,24},{24,28},{1,5},{5,9},{9,... | collective-permute-start | bytes 1572872 | tf_op jit(solution)/shard_map/ppermute | solution.py:19
  74.1 1.5 collective-permute-done.5
  78.0 4.9 collective-permute-start.7
  82.9 2.6 collective-permute-done.6
  85.5 1.5 collective-permute-done.7
  86.9 24.8 %fusion.87 = f32[16,16,32,256]{3,0,2,1:T(8,128)} fusion(f32[16,16,32,256]{3,0,2,1:T(8,128)} %fusion.81, f32[16,1,32,256]{3,0,2,1:T(8,128)S(1)} %collective-permute-done.4, f32[16,1,32,256]{3,0,2,1:T(8,128)S(1)} %collective-permute-done.5, f32[16,18,1,256]{3,0,2,1:T(8,128)S(1)} %collective-permute-done.7, f32[16,18,1,256]{3,0,2,1:T(8,128)S(1)} %collective-permute-done.6, ...), kind=kLoop, calls=%fused_computation.164 | loop fusion | flops 50331648 | bytes 27983884 | tf_op jit(solution)/shard_map/jit(_where)/select_n | solution.py:42
  114.4 12.9 %collective-permute-start.9 = (f32[16,1,32,256]{3,0,2,1:T(8,128)S(1)}, f32[16,1,32,256]{3,0,2,1:T(8,128)S(1)}, u32[]{:S(2)}, u32[]{:S(2)}) collective-permute-start(f32[16,1,32,256]{3,0,2,1:T(8,128)S(1)} %get-tuple-element.38), channel_id=1, source_target_pairs={{0,4},{4,8},{8,12},{12,16},{16,20},{20,24},{24,28},{1,5},{5,9},{9,... | collective-permute-start | bytes 1572872 | tf_op jit(solution)/shard_map/ppermute | solution.py:19
  127.3 1.5 collective-permute-done.9
  131.2 4.7 collective-permute-start.11
  135.9 2.7 collective-permute-done.10
  140.1 24.8 %fusion.86 = f32[16,16,32,256]{3,0,2,1:T(8,128)} fusion(f32[16,16,32,256]{3,0,2,1:T(8,128)} %fusion.87, f32[16,1,32,256]{3,0,2,1:T(8,128)S(1)} %collective-permute-done.8, f32[16,1,32,256]{3,0,2,1:T(8,128)S(1)} %collective-permute-done.9, f32[16,18,1,256]{3,0,2,1:T(8,128)S(1)} %collective-permute-done.11, ...), kind=kLoop, calls=%fused_computation.163 | loop fusion | flops 50331648 | bytes 27983884 | tf_op jit(solution)/shard_map/jit(_where)/select_n | solution.py:42
  167.4 10.1 %collective-permute-start.13 = (f32[16,1,32,256]{3,0,2,1:T(8,128)S(1)}, f32[16,1,32,256]{3,0,2,1:T(8,128)S(1)}, u32[]{:S(2)}, u32[]{:S(2)}) collective-permute-start(f32[16,1,32,256]{3,0,2,1:T(8,128)S(1)} %get-tuple-element.36), channel_id=1, source_target_pairs={{0,4},{4,8},{8,12},{12,16},{16,20},{20,24},{24,28},{1,5},{5,9},{9,... | collective-permute-start | bytes 1572872 | tf_op jit(solution)/shard_map/ppermute | solution.py:19
  177.6 1.5 collective-permute-done.13
  181.4 4.8 collective-permute-start.15
  186.3 2.7 collective-permute-done.14
  189.0 1.5 collective-permute-done.15
  190.5 24.2 %fusion.85 = f32[16,16,32,256]{3,0,2,1:T(8,128)S(1)} fusion(f32[16,16,32,256]{3,0,2,1:T(8,128)} %fusion.86, f32[16,1,32,256]{3,0,2,1:T(8,128)S(1)} %collective-permute-done.12, f32[16,1,32,256]{3,0,2,1:T(8,128)S(1)} %collective-permute-done.13, f32[16,18,1,256]{3,0,2,1:T(8,128)S(1)} %collective-permute-done.15, ...), kind=kLoop, calls=%fused_computation.162 | loop fusion | flops 50331648 | bytes 27983884 | tf_op jit(solution)/shard_map/jit(_where)/select_n | solution.py:42
  216.1 9.8 %collective-permute-start.17 = (f32[16,1,32,256]{3,0,2,1:T(8,128)S(1)}, f32[16,1,32,256]{3,0,2,1:T(8,128)S(1)}, u32[]{:S(2)}, u32[]{:S(2)}) collective-permute-start(f32[16,1,32,256]{3,0,2,1:T(8,128)S(1)} %get-tuple-element.34), channel_id=1, source_target_pairs={{0,4},{4,8},{8,12},{12,16},{16,20},{20,24},{24,28},{1,5},{5,9},{9,... | collective-permute-start | bytes 1572872 | tf_op jit(solution)/shard_map/ppermute | solution.py:19
  225.9 1.5 collective-permute-done.17
  228.7 5.1 collective-permute-start.19
  233.8 2.5 collective-permute-done.18
  237.8 13.1 %fusion.80 = f32[16,16,32,256]{3,0,2,1:T(8,128)} fusion(f32[16,16,32,256]{3,0,2,1:T(8,128)S(1)} %fusion.85, f32[16,1,32,256]{3,0,2,1:T(8,128)S(1)} %collective-permute-done.16, f32[16,1,32,256]{3,0,2,1:T(8,128)S(1)} %collective-permute-done.17, f32[16,18,1,256]{3,0,2,1:T(8,128)S(1)} %collective-permute-done.19, ...), kind=kLoop, calls=%fused_computation.157 | loop fusion | flops 50331648 | bytes 19595276 | tf_op jit(solution)/shard_map/jit(_where)/select_n | solution.py:42
  253.5 9.8 %collective-permute-start.21 = (f32[16,1,32,256]{3,0,2,1:T(8,128)S(1)}, f32[16,1,32,256]{3,0,2,1:T(8,128)S(1)}, u32[]{:S(2)}, u32[]{:S(2)}) collective-permute-start(f32[16,1,32,256]{3,0,2,1:T(8,128)S(1)} %get-tuple-element.32), channel_id=1, source_target_pairs={{0,4},{4,8},{8,12},{12,16},{16,20},{20,24},{24,28},{1,5},{5,9},{9,... | collective-permute-start | bytes 1572872 | tf_op jit(solution)/shard_map/ppermute | solution.py:19
  263.3 1.5 collective-permute-done.21
  267.1 4.8 collective-permute-start.23
  272.0 2.7 collective-permute-done.22
  276.2 22.7 %fusion.84 = f32[16,16,32,256]{3,0,2,1:T(8,128)} fusion(f32[16,16,32,256]{3,0,2,1:T(8,128)S(1)} %fusion.85, f32[16,16,32,256]{3,0,2,1:T(8,128)} %fusion.80, f32[16,1,32,256]{3,0,2,1:T(8,128)S(1)} %collective-permute-done.20, f32[16,1,32,256]{3,0,2,1:T(8,128)S(1)} %collective-permute-done.21, f32[16,18,1,256]{3,0,2,1:T(8,128)S(1)} %collective-permute-done.23, ...), kind=kLoop, calls=%fused_computation.161 | loop fusion | flops 50331648 | bytes 27983884 | tf_op jit(solution)/shard_map/jit(_where)/select_n | solution.py:42
  301.5 11.3 %collective-permute-start.25 = (f32[16,1,32,256]{3,0,2,1:T(8,128)S(1)}, f32[16,1,32,256]{3,0,2,1:T(8,128)S(1)}, u32[]{:S(2)}, u32[]{:S(2)}) collective-permute-start(f32[16,1,32,256]{3,0,2,1:T(8,128)S(1)} %get-tuple-element.30), channel_id=1, source_target_pairs={{0,4},{4,8},{8,12},{12,16},{16,20},{20,24},{24,28},{1,5},{5,9},{9,... | collective-permute-start | bytes 1572872 | tf_op jit(solution)/shard_map/ppermute | solution.py:19
  312.8 1.5 collective-permute-done.25
  316.7 4.7 collective-permute-start.27
  322.1 2.1 collective-permute-done.26
  325.6 22.7 %fusion.83 = f32[16,16,32,256]{3,0,2,1:T(8,128)} fusion(f32[16,16,32,256]{3,0,2,1:T(8,128)S(1)} %fusion.85, f32[16,16,32,256]{3,0,2,1:T(8,128)} %fusion.84, f32[16,1,32,256]{3,0,2,1:T(8,128)S(1)} %collective-permute-done.24, f32[16,1,32,256]{3,0,2,1:T(8,128)S(1)} %collective-permute-done.25, f32[16,18,1,256]{3,0,2,1:T(8,128)S(1)} %collective-permute-done.27, ...), kind=kLoop, calls=%fused_computation.160 | loop fusion | flops 50331648 | bytes 27983884 | tf_op jit(solution)/shard_map/jit(_where)/select_n | solution.py:42
  350.9 13.9 %collective-permute-start.29 = (f32[16,1,32,256]{3,0,2,1:T(8,128)S(1)}, f32[16,1,32,256]{3,0,2,1:T(8,128)S(1)}, u32[]{:S(2)}, u32[]{:S(2)}) collective-permute-start(f32[16,1,32,256]{3,0,2,1:T(8,128)S(1)} %get-tuple-element.28), channel_id=1, source_target_pairs={{0,4},{4,8},{8,12},{12,16},{16,20},{20,24},{24,28},{1,5},{5,9},{9,... | collective-permute-start | bytes 1572872 | tf_op jit(solution)/shard_map/ppermute | solution.py:19
  368.7 4.7 collective-permute-start.31
  373.5 2.7 collective-permute-done.30
  377.7 22.7 %fusion.82 = f32[16,16,32,256]{3,0,2,1:T(8,128)} fusion(f32[16,16,32,256]{3,0,2,1:T(8,128)S(1)} %fusion.85, f32[16,16,32,256]{3,0,2,1:T(8,128)} %fusion.83, f32[16,1,32,256]{3,0,2,1:T(8,128)S(1)} %collective-permute-done.28, f32[16,1,32,256]{3,0,2,1:T(8,128)S(1)} %collective-permute-done.29, f32[16,18,1,256]{3,0,2,1:T(8,128)S(1)} %collective-permute-done.31, ...), kind=kLoop, calls=%fused_computation.159 | loop fusion | flops 50331648 | bytes 27983884 | tf_op jit(solution)/shard_map/jit(_where)/select_n | solution.py:42
  400.4 32.9 %copy.61 = f32[16,16,32,256]{0,3,2,1:T(8,128)} copy(f32[16,16,32,256]{3,0,2,1:T(8,128)} %fusion.82) | data formatting | bytes 16777216 | tf_op jit(solution)/shard_map/jit(_where)/select_n | solution.py:42
  433.3 1.8 gather_fusion
  436.0 39.7 %all-to-all-start = ((f32[32,1,128]{2,1,0:T(1,128)}), f32[32,1,128]{2,1,0:T(1,128)S(1)}, u32[]{:S(2)}, u32[]{:S(2)}) async-start(f32[32,1,128]{2,1,0:T(1,128)} %reshape.93), calls=%async_computation | async-start | bytes 32768 | tf_op jit(solution)/shard_map/all_to_all | solution.py:74
  475.7 11.6 %copy.66 = f32[16,16,32,256]{3,2,1,0:T(8,128)} copy(f32[16,16,32,256]{3,0,2,1:T(8,128)} %fusion.82) | data formatting | bytes 16777216
  489.2 40.6 %psum.7 = f32[16,16]{1,0:T(8,128)} all-reduce(f32[16,16]{1,0:T(8,128)S(1)} %fusion.109), channel_id=1, replica_groups=mesh['gx'=8,'gy'=4] {'gx','gy'}, use_global_device_ids=true, to_apply=%region_1.2 | all-reduce | flops 256 | bytes 2048 | tf_op jit(solution)/shard_map/psum | solution.py:81
  (84 shorter events, 50.1 us)
Async XLA Ops:
  0.6 15.4 %copy-start = (f32[16,16,32,256]{3,2,1,0:T(8,128)S(1)}, f32[16,16,32,256]{3,2,1,0:T(8,128)}, u32[]{:S(2)}) copy-start(f32[16,16,32,256]{3,2,1,0:T(8,128)} %param.7) | copy-start | bytes 25165828
  0.6 14.4 %copy-start.1 = (f32[16,32,256]{2,1,0:T(8,128)S(1)}, f32[16,32,256]{2,1,0:T(8,128)}, u32[]{:S(2)}) copy-start(f32[16,32,256]{2,1,0:T(8,128)} %param.8) | copy-start | bytes 1572868
  10.7 15.3 %copy-start.2 = (f32[16,16,32,256]{3,0,2,1:T(8,128)}, f32[16,16,32,256]{3,0,2,1:T(8,128)S(1)}, u32[]{:S(2)}) copy-start(f32[16,16,32,256]{3,0,2,1:T(8,128)S(1)} %copy.60) | copy-start | bytes 25165828
  10.8 4.4 collective-permute-start.1
  13.3 12.8 %collective-permute-start = (f32[16,1,32,256]{3,0,2,1:T(8,128)S(1)}, f32[16,1,32,256]{3,0,2,1:T(8,128)S(1)}, u32[]{:S(2)}, u32[]{:S(2)}) collective-permute-start(f32[16,1,32,256]{3,0,2,1:T(8,128)S(1)} %get-tuple-element.42), channel_id=1, source_target_pairs={{4,0},{8,4},{12,8},{16,12},{20,16},{24,20},{28,24},{5,1},{9,5},{13... | collective-permute-start | bytes 1572872 | tf_op jit(solution)/shard_map/ppermute | solution.py:21
  16.0 18.2 %copy-start.5 = (f32[3]{0:T(128)S(1)}, f32[3]{0:T(128)}, u32[]{:S(2)}) copy-start(f32[3]{0:T(128)} %param.9) | copy-start | bytes 40
  28.0 9.0 %collective-permute-start.2 = (f32[16,18,1,256]{3,0,2,1:T(8,128)S(1)}, f32[16,18,1,256]{3,0,2,1:T(8,128)S(1)}, u32[]{:S(2)}, u32[]{:S(2)}) collective-permute-start(f32[16,18,1,256]{3,0,2,1:T(8,128)S(1)} %get-tuple-element.26), channel_id=1, source_target_pairs={{1,0},{2,1},{3,2},{5,4},{6,5},{7,6},{9,8},{10,9},{11,10},{13,12},{... | collective-permute-start | bytes 884744 | tf_op jit(solution)/shard_map/ppermute | solution.py:21
  29.3 9.2 %collective-permute-start.3 = (f32[16,18,1,256]{3,0,2,1:T(8,128)S(1)}, f32[16,18,1,256]{3,0,2,1:T(8,128)S(1)}, u32[]{:S(2)}, u32[]{:S(2)}) collective-permute-start(f32[16,18,1,256]{3,0,2,1:T(8,128)S(1)} %get-tuple-element.27), channel_id=1, source_target_pairs={{0,1},{1,2},{2,3},{4,5},{5,6},{6,7},{8,9},{9,10},{10,11},{12,13},{... | collective-permute-start | bytes 884744 | tf_op jit(solution)/shard_map/ppermute | solution.py:19
  65.0 9.1 %collective-permute-start.4 = (f32[16,1,32,256]{3,0,2,1:T(8,128)S(1)}, f32[16,1,32,256]{3,0,2,1:T(8,128)S(1)}, u32[]{:S(2)}, u32[]{:S(2)}) collective-permute-start(f32[16,1,32,256]{3,0,2,1:T(8,128)S(1)} %get-tuple-element.41), channel_id=1, source_target_pairs={{4,0},{8,4},{12,8},{16,12},{20,16},{24,20},{28,24},{5,1},{9,5},{13... | collective-permute-start | bytes 1572872 | tf_op jit(solution)/shard_map/ppermute | solution.py:21
  66.3 9.3 %collective-permute-start.5 = (f32[16,1,32,256]{3,0,2,1:T(8,128)S(1)}, f32[16,1,32,256]{3,0,2,1:T(8,128)S(1)}, u32[]{:S(2)}, u32[]{:S(2)}) collective-permute-start(f32[16,1,32,256]{3,0,2,1:T(8,128)S(1)} %get-tuple-element.40), channel_id=1, source_target_pairs={{0,4},{4,8},{8,12},{12,16},{16,20},{20,24},{24,28},{1,5},{5,9},{9,... | collective-permute-start | bytes 1572872 | tf_op jit(solution)/shard_map/ppermute | solution.py:19
  76.7 8.8 %collective-permute-start.6 = (f32[16,18,1,256]{3,0,2,1:T(8,128)S(1)}, f32[16,18,1,256]{3,0,2,1:T(8,128)S(1)}, u32[]{:S(2)}, u32[]{:S(2)}) collective-permute-start(f32[16,18,1,256]{3,0,2,1:T(8,128)S(1)} %get-tuple-element.24), channel_id=1, source_target_pairs={{1,0},{2,1},{3,2},{5,4},{6,5},{7,6},{9,8},{10,9},{11,10},{13,12},{... | collective-permute-start | bytes 884744 | tf_op jit(solution)/shard_map/ppermute | solution.py:21
  78.0 8.9 %collective-permute-start.7 = (f32[16,18,1,256]{3,0,2,1:T(8,128)S(1)}, f32[16,18,1,256]{3,0,2,1:T(8,128)S(1)}, u32[]{:S(2)}, u32[]{:S(2)}) collective-permute-start(f32[16,18,1,256]{3,0,2,1:T(8,128)S(1)} %get-tuple-element.25), channel_id=1, source_target_pairs={{0,1},{1,2},{2,3},{4,5},{5,6},{6,7},{8,9},{9,10},{10,11},{12,13},{... | collective-permute-start | bytes 884744 | tf_op jit(solution)/shard_map/ppermute | solution.py:19
  113.1 14.2 %collective-permute-start.8 = (f32[16,1,32,256]{3,0,2,1:T(8,128)S(1)}, f32[16,1,32,256]{3,0,2,1:T(8,128)S(1)}, u32[]{:S(2)}, u32[]{:S(2)}) collective-permute-start(f32[16,1,32,256]{3,0,2,1:T(8,128)S(1)} %get-tuple-element.39), channel_id=1, source_target_pairs={{4,0},{8,4},{12,8},{16,12},{20,16},{24,20},{28,24},{5,1},{9,5},{13... | collective-permute-start | bytes 1572872 | tf_op jit(solution)/shard_map/ppermute | solution.py:21
  114.4 14.4 %collective-permute-start.9 = (f32[16,1,32,256]{3,0,2,1:T(8,128)S(1)}, f32[16,1,32,256]{3,0,2,1:T(8,128)S(1)}, u32[]{:S(2)}, u32[]{:S(2)}) collective-permute-start(f32[16,1,32,256]{3,0,2,1:T(8,128)S(1)} %get-tuple-element.38), channel_id=1, source_target_pairs={{0,4},{4,8},{8,12},{12,16},{16,20},{20,24},{24,28},{1,5},{5,9},{9,... | collective-permute-start | bytes 1572872 | tf_op jit(solution)/shard_map/ppermute | solution.py:19
  129.9 8.8 %collective-permute-start.10 = (f32[16,18,1,256]{3,0,2,1:T(8,128)S(1)}, f32[16,18,1,256]{3,0,2,1:T(8,128)S(1)}, u32[]{:S(2)}, u32[]{:S(2)}) collective-permute-start(f32[16,18,1,256]{3,0,2,1:T(8,128)S(1)} %get-tuple-element.22), channel_id=1, source_target_pairs={{1,0},{2,1},{3,2},{5,4},{6,5},{7,6},{9,8},{10,9},{11,10},{13,12},{... | collective-permute-start | bytes 884744 | tf_op jit(solution)/shard_map/ppermute | solution.py:21
  131.2 8.9 %collective-permute-start.11 = (f32[16,18,1,256]{3,0,2,1:T(8,128)S(1)}, f32[16,18,1,256]{3,0,2,1:T(8,128)S(1)}, u32[]{:S(2)}, u32[]{:S(2)}) collective-permute-start(f32[16,18,1,256]{3,0,2,1:T(8,128)S(1)} %get-tuple-element.23), channel_id=1, source_target_pairs={{0,1},{1,2},{2,3},{4,5},{5,6},{6,7},{8,9},{9,10},{10,11},{12,13},{... | collective-permute-start | bytes 884744 | tf_op jit(solution)/shard_map/ppermute | solution.py:19
  166.1 11.4 %collective-permute-start.12 = (f32[16,1,32,256]{3,0,2,1:T(8,128)S(1)}, f32[16,1,32,256]{3,0,2,1:T(8,128)S(1)}, u32[]{:S(2)}, u32[]{:S(2)}) collective-permute-start(f32[16,1,32,256]{3,0,2,1:T(8,128)S(1)} %get-tuple-element.37), channel_id=1, source_target_pairs={{4,0},{8,4},{12,8},{16,12},{20,16},{24,20},{28,24},{5,1},{9,5},{13... | collective-permute-start | bytes 1572872 | tf_op jit(solution)/shard_map/ppermute | solution.py:21
  167.4 11.6 %collective-permute-start.13 = (f32[16,1,32,256]{3,0,2,1:T(8,128)S(1)}, f32[16,1,32,256]{3,0,2,1:T(8,128)S(1)}, u32[]{:S(2)}, u32[]{:S(2)}) collective-permute-start(f32[16,1,32,256]{3,0,2,1:T(8,128)S(1)} %get-tuple-element.36), channel_id=1, source_target_pairs={{0,4},{4,8},{8,12},{12,16},{16,20},{20,24},{24,28},{1,5},{5,9},{9,... | collective-permute-start | bytes 1572872 | tf_op jit(solution)/shard_map/ppermute | solution.py:19
  180.1 8.9 %collective-permute-start.14 = (f32[16,18,1,256]{3,0,2,1:T(8,128)S(1)}, f32[16,18,1,256]{3,0,2,1:T(8,128)S(1)}, u32[]{:S(2)}, u32[]{:S(2)}) collective-permute-start(f32[16,18,1,256]{3,0,2,1:T(8,128)S(1)} %get-tuple-element.20), channel_id=1, source_target_pairs={{1,0},{2,1},{3,2},{5,4},{6,5},{7,6},{9,8},{10,9},{11,10},{13,12},{... | collective-permute-start | bytes 884744 | tf_op jit(solution)/shard_map/ppermute | solution.py:21
  181.4 9.1 %collective-permute-start.15 = (f32[16,18,1,256]{3,0,2,1:T(8,128)S(1)}, f32[16,18,1,256]{3,0,2,1:T(8,128)S(1)}, u32[]{:S(2)}, u32[]{:S(2)}) collective-permute-start(f32[16,18,1,256]{3,0,2,1:T(8,128)S(1)} %get-tuple-element.21), channel_id=1, source_target_pairs={{0,1},{1,2},{2,3},{4,5},{5,6},{6,7},{8,9},{9,10},{10,11},{12,13},{... | collective-permute-start | bytes 884744 | tf_op jit(solution)/shard_map/ppermute | solution.py:19
  214.8 11.1 %collective-permute-start.16 = (f32[16,1,32,256]{3,0,2,1:T(8,128)S(1)}, f32[16,1,32,256]{3,0,2,1:T(8,128)S(1)}, u32[]{:S(2)}, u32[]{:S(2)}) collective-permute-start(f32[16,1,32,256]{3,0,2,1:T(8,128)S(1)} %get-tuple-element.35), channel_id=1, source_target_pairs={{4,0},{8,4},{12,8},{16,12},{20,16},{24,20},{28,24},{5,1},{9,5},{13... | collective-permute-start | bytes 1572872 | tf_op jit(solution)/shard_map/ppermute | solution.py:21
  216.1 11.3 %collective-permute-start.17 = (f32[16,1,32,256]{3,0,2,1:T(8,128)S(1)}, f32[16,1,32,256]{3,0,2,1:T(8,128)S(1)}, u32[]{:S(2)}, u32[]{:S(2)}) collective-permute-start(f32[16,1,32,256]{3,0,2,1:T(8,128)S(1)} %get-tuple-element.34), channel_id=1, source_target_pairs={{0,4},{4,8},{8,12},{12,16},{16,20},{20,24},{24,28},{1,5},{5,9},{9,... | collective-permute-start | bytes 1572872 | tf_op jit(solution)/shard_map/ppermute | solution.py:19
  227.4 8.9 %collective-permute-start.18 = (f32[16,18,1,256]{3,0,2,1:T(8,128)S(1)}, f32[16,18,1,256]{3,0,2,1:T(8,128)S(1)}, u32[]{:S(2)}, u32[]{:S(2)}) collective-permute-start(f32[16,18,1,256]{3,0,2,1:T(8,128)S(1)} %get-tuple-element.18), channel_id=1, source_target_pairs={{1,0},{2,1},{3,2},{5,4},{6,5},{7,6},{9,8},{10,9},{11,10},{13,12},{... | collective-permute-start | bytes 884744 | tf_op jit(solution)/shard_map/ppermute | solution.py:21
  228.7 9.1 %collective-permute-start.19 = (f32[16,18,1,256]{3,0,2,1:T(8,128)S(1)}, f32[16,18,1,256]{3,0,2,1:T(8,128)S(1)}, u32[]{:S(2)}, u32[]{:S(2)}) collective-permute-start(f32[16,18,1,256]{3,0,2,1:T(8,128)S(1)} %get-tuple-element.19), channel_id=1, source_target_pairs={{0,1},{1,2},{2,3},{4,5},{5,6},{6,7},{8,9},{9,10},{10,11},{12,13},{... | collective-permute-start | bytes 884744 | tf_op jit(solution)/shard_map/ppermute | solution.py:19
  252.2 11.1 %collective-permute-start.20 = (f32[16,1,32,256]{3,0,2,1:T(8,128)S(1)}, f32[16,1,32,256]{3,0,2,1:T(8,128)S(1)}, u32[]{:S(2)}, u32[]{:S(2)}) collective-permute-start(f32[16,1,32,256]{3,0,2,1:T(8,128)S(1)} %get-tuple-element.33), channel_id=1, source_target_pairs={{4,0},{8,4},{12,8},{16,12},{20,16},{24,20},{28,24},{5,1},{9,5},{13... | collective-permute-start | bytes 1572872 | tf_op jit(solution)/shard_map/ppermute | solution.py:21
  253.5 11.3 %collective-permute-start.21 = (f32[16,1,32,256]{3,0,2,1:T(8,128)S(1)}, f32[16,1,32,256]{3,0,2,1:T(8,128)S(1)}, u32[]{:S(2)}, u32[]{:S(2)}) collective-permute-start(f32[16,1,32,256]{3,0,2,1:T(8,128)S(1)} %get-tuple-element.32), channel_id=1, source_target_pairs={{0,4},{4,8},{8,12},{12,16},{16,20},{20,24},{24,28},{1,5},{5,9},{9,... | collective-permute-start | bytes 1572872 | tf_op jit(solution)/shard_map/ppermute | solution.py:19
  265.8 8.9 %collective-permute-start.22 = (f32[16,18,1,256]{3,0,2,1:T(8,128)S(1)}, f32[16,18,1,256]{3,0,2,1:T(8,128)S(1)}, u32[]{:S(2)}, u32[]{:S(2)}) collective-permute-start(f32[16,18,1,256]{3,0,2,1:T(8,128)S(1)} %get-tuple-element.16), channel_id=1, source_target_pairs={{1,0},{2,1},{3,2},{5,4},{6,5},{7,6},{9,8},{10,9},{11,10},{13,12},{... | collective-permute-start | bytes 884744 | tf_op jit(solution)/shard_map/ppermute | solution.py:21
  267.1 9.1 %collective-permute-start.23 = (f32[16,18,1,256]{3,0,2,1:T(8,128)S(1)}, f32[16,18,1,256]{3,0,2,1:T(8,128)S(1)}, u32[]{:S(2)}, u32[]{:S(2)}) collective-permute-start(f32[16,18,1,256]{3,0,2,1:T(8,128)S(1)} %get-tuple-element.17), channel_id=1, source_target_pairs={{0,1},{1,2},{2,3},{4,5},{5,6},{6,7},{8,9},{9,10},{10,11},{12,13},{... | collective-permute-start | bytes 884744 | tf_op jit(solution)/shard_map/ppermute | solution.py:19
  300.2 12.6 %collective-permute-start.24 = (f32[16,1,32,256]{3,0,2,1:T(8,128)S(1)}, f32[16,1,32,256]{3,0,2,1:T(8,128)S(1)}, u32[]{:S(2)}, u32[]{:S(2)}) collective-permute-start(f32[16,1,32,256]{3,0,2,1:T(8,128)S(1)} %get-tuple-element.31), channel_id=1, source_target_pairs={{4,0},{8,4},{12,8},{16,12},{20,16},{24,20},{28,24},{5,1},{9,5},{13... | collective-permute-start | bytes 1572872 | tf_op jit(solution)/shard_map/ppermute | solution.py:21
  301.5 12.8 %collective-permute-start.25 = (f32[16,1,32,256]{3,0,2,1:T(8,128)S(1)}, f32[16,1,32,256]{3,0,2,1:T(8,128)S(1)}, u32[]{:S(2)}, u32[]{:S(2)}) collective-permute-start(f32[16,1,32,256]{3,0,2,1:T(8,128)S(1)} %get-tuple-element.30), channel_id=1, source_target_pairs={{0,4},{4,8},{8,12},{12,16},{16,20},{20,24},{24,28},{1,5},{5,9},{9,... | collective-permute-start | bytes 1572872 | tf_op jit(solution)/shard_map/ppermute | solution.py:19
  315.4 8.8 %collective-permute-start.26 = (f32[16,18,1,256]{3,0,2,1:T(8,128)S(1)}, f32[16,18,1,256]{3,0,2,1:T(8,128)S(1)}, u32[]{:S(2)}, u32[]{:S(2)}) collective-permute-start(f32[16,18,1,256]{3,0,2,1:T(8,128)S(1)} %get-tuple-element.14), channel_id=1, source_target_pairs={{1,0},{2,1},{3,2},{5,4},{6,5},{7,6},{9,8},{10,9},{11,10},{13,12},{... | collective-permute-start | bytes 884744 | tf_op jit(solution)/shard_map/ppermute | solution.py:21
  316.7 8.9 %collective-permute-start.27 = (f32[16,18,1,256]{3,0,2,1:T(8,128)S(1)}, f32[16,18,1,256]{3,0,2,1:T(8,128)S(1)}, u32[]{:S(2)}, u32[]{:S(2)}) collective-permute-start(f32[16,18,1,256]{3,0,2,1:T(8,128)S(1)} %get-tuple-element.15), channel_id=1, source_target_pairs={{0,1},{1,2},{2,3},{4,5},{5,6},{6,7},{8,9},{9,10},{10,11},{12,13},{... | collective-permute-start | bytes 884744 | tf_op jit(solution)/shard_map/ppermute | solution.py:19
  322.1 42.8 %copy-start.7 = (s32[1,1,128,1]{2,3,1,0:T(1,128)S(1)}, s32[1,1,128,1]{2,3,1,0:T(1,128)}, u32[]{:S(2)}) copy-start(s32[1,1,128,1]{2,3,1,0:T(1,128)} %param.11) | copy-start | bytes 1540
  322.1 43.0 %copy-start.6 = (s32[1,1,128]{2,1,0:T(1,128)S(1)}, s32[1,1,128]{2,1,0:T(1,128)}, u32[]{:S(2)}) copy-start(s32[1,1,128]{2,1,0:T(1,128)} %param.10) | copy-start | bytes 1540
  349.6 15.5 %collective-permute-start.28 = (f32[16,1,32,256]{3,0,2,1:T(8,128)S(1)}, f32[16,1,32,256]{3,0,2,1:T(8,128)S(1)}, u32[]{:S(2)}, u32[]{:S(2)}) collective-permute-start(f32[16,1,32,256]{3,0,2,1:T(8,128)S(1)} %get-tuple-element.29), channel_id=1, source_target_pairs={{4,0},{8,4},{12,8},{16,12},{20,16},{24,20},{28,24},{5,1},{9,5},{13... | collective-permute-start | bytes 1572872 | tf_op jit(solution)/shard_map/ppermute | solution.py:21
  350.9 15.4 %collective-permute-start.29 = (f32[16,1,32,256]{3,0,2,1:T(8,128)S(1)}, f32[16,1,32,256]{3,0,2,1:T(8,128)S(1)}, u32[]{:S(2)}, u32[]{:S(2)}) collective-permute-start(f32[16,1,32,256]{3,0,2,1:T(8,128)S(1)} %get-tuple-element.28), channel_id=1, source_target_pairs={{0,4},{4,8},{8,12},{12,16},{16,20},{20,24},{24,28},{1,5},{5,9},{9,... | collective-permute-start | bytes 1572872 | tf_op jit(solution)/shard_map/ppermute | solution.py:19
  367.4 8.8 %collective-permute-start.30 = (f32[16,18,1,256]{3,0,2,1:T(8,128)S(1)}, f32[16,18,1,256]{3,0,2,1:T(8,128)S(1)}, u32[]{:S(2)}, u32[]{:S(2)}) collective-permute-start(f32[16,18,1,256]{3,0,2,1:T(8,128)S(1)} %get-tuple-element.12), channel_id=1, source_target_pairs={{1,0},{2,1},{3,2},{5,4},{6,5},{7,6},{9,8},{10,9},{11,10},{13,12},{... | collective-permute-start | bytes 884744 | tf_op jit(solution)/shard_map/ppermute | solution.py:21
  368.7 8.9 %collective-permute-start.31 = (f32[16,18,1,256]{3,0,2,1:T(8,128)S(1)}, f32[16,18,1,256]{3,0,2,1:T(8,128)S(1)}, u32[]{:S(2)}, u32[]{:S(2)}) collective-permute-start(f32[16,18,1,256]{3,0,2,1:T(8,128)S(1)} %get-tuple-element.13), channel_id=1, source_target_pairs={{0,1},{1,2},{2,3},{4,5},{5,6},{6,7},{8,9},{9,10},{10,11},{12,13},{... | collective-permute-start | bytes 884744 | tf_op jit(solution)/shard_map/ppermute | solution.py:19
  400.4 34.7 %copy-start.4 = (f32[1,1,128,16]{2,3,1,0:T(8,128)S(1)}, f32[1,1,128,16]{2,3,1,0:T(8,128)}, u32[]{:S(2)}) copy-start(f32[1,1,128,16]{2,3,1,0:T(8,128)} %param.13) | copy-start | bytes 24580
  436.0 51.3 %all-to-all-start = ((f32[32,1,128]{2,1,0:T(1,128)}), f32[32,1,128]{2,1,0:T(1,128)S(1)}, u32[]{:S(2)}, u32[]{:S(2)}) async-start(f32[32,1,128]{2,1,0:T(1,128)} %reshape.93), calls=%async_computation | async-start | bytes 32768 | tf_op jit(solution)/shard_map/all_to_all | solution.py:74
  488.9 40.8 %copy-start.3 = (f32[16,16]{1,0:T(8,128)}, f32[16,16]{1,0:T(8,128)S(1)}, u32[]{:S(2)}) copy-start(f32[16,16]{1,0:T(8,128)S(1)} %convolution_bitcast_fusion) | copy-start | bytes 3076
where the time goes:
time: 538 us; the launch traced here: 530 us
  other arithmetic  190 us (35%)
  starting transfers between devices  178 us (33%)
  local copies, waits for them, and re-layouts  79 us (15%)
  blocking collectives  40.6 us (8%)
  waiting for transfers between devices  39.9 us (7%)
    select_n x8, other arithmetic, relax(): return jnp.where(diffusion > 0.0, updated, 0.0)  180 us
    ppermute x16, starting transfers between devices, padded_2(): lax.ppermute(tail, axis, [(i, (i + 1) % count) for i in range(ends)])  117 us
    psum x1, blocking collectives, body(): lax.psum(jnp.dot(goal_block.T, goal_block, precision=lax.Precision.HIGHES...  40.6 us
    all_to_all x1, starting transfers between devices, body(): lax.all_to_all(outgoing, ('gx', 'gy'), split_axis=0, concat_axis=0, tiled...  39.7 us
    unnamed x22, local copies, waits for them, and re-layouts  33.4 us
    select_n x1, local copies, waits for them, and re-layouts, relax(): return jnp.where(diffusion > 0.0, updated, 0.0)  32.9 us
    ppermute x16, waiting for transfers between devices, padded_2(): lax.ppermute(tail, axis, [(i, (i + 1) % count) for i in range(ends)])  21.8 us
    ppermute x16, starting transfers between devices, padded_2(): lax.ppermute(head, axis, [((i + 1) % count, i) for i in range(ends)])  21.2 us
  transfers between devices with their start and end apart: 33, of which 22 were waited for; matrix products, arithmetic and copies ran while one was open for 5% of the time, Pallas kernels for 0%

commit v1 on v0

--- a/solution.py
+++ b/solution.py
@@ -78,8 +78,11 @@
         received[..., :probe_count],
         precision=lax.Precision.HIGHEST,
     )
-    ritz_gram = lax.psum(
-        jnp.dot(goal_block.T, goal_block, precision=lax.Precision.HIGHEST), ("gx", "gy")
+    ritz_gram = jnp.sum(
+        lax.all_gather(
+            jnp.dot(goal_block.T, goal_block, precision=lax.Precision.HIGHEST), ("gx", "gy")
+        ),
+        axis=0,
     )
     return (state_field, goal_block, ritz_gram)
 

time: 538 us -> 568 us (1.056)
  blocking collectives: 40.6 us -> 70.7 us
    all_gather x0 -> x1, blocking collectives: none -> 70.7 us  [body(): lax.all_gather(jnp.dot(goal_block.T, goal_block, precision=lax.Precision....]
    psum x1 -> x0, blocking collectives: 40.6 us -> none  [body(): lax.psum(jnp.dot(goal_block.T, goal_block, precision=lax.Precision.HIGHES...]
where the time goes in v1:
time: 568 us; the launch traced here: 561 us
  other arithmetic  191 us (34%)
  starting transfers between devices  178 us (31%)
  local copies, waits for them, and re-layouts  79 us (14%)
  blocking collectives  70.7 us (12%)
  waiting for transfers between devices  39.9 us (7%)
    select_n x8, other arithmetic, relax(): return jnp.where(diffusion > 0.0, updated, 0.0)  180 us
    ppermute x16, starting transfers between devices, padded_2(): lax.ppermute(tail, axis, [(i, (i + 1) % count) for i in range(ends)])  117 us
    all_gather x1, blocking collectives, body(): lax.all_gather(jnp.dot(goal_block.T, goal_block, precision=lax.Precision....  70.7 us
    all_to_all x1, starting transfers between devices, body(): lax.all_to_all(outgoing, ('gx', 'gy'), split_axis=0, concat_axis=0, tiled...  39.7 us
    unnamed x22, local copies, waits for them, and re-layouts  33.4 us
    select_n x1, local copies, waits for them, and re-layouts, relax(): return jnp.where(diffusion > 0.0, updated, 0.0)  32.9 us
    ppermute x16, waiting for transfers between devices, padded_2(): lax.ppermute(tail, axis, [(i, (i + 1) % count) for i in range(ends)])  21.8 us
    ppermute x16, starting transfers between devices, padded_2(): lax.ppermute(head, axis, [((i + 1) % count, i) for i in range(ends)])  21.2 us
  transfers between devices with their start and end apart: 33, of which 22 were waited for; matrix products, arithmetic and copies ran while one was open for 5% of the time, Pallas kernels for 0%

profile of v1, /device:TPU:0, one launch (start us, length us, event | category | flops | bytes accessed | tf_op | source)
XLA Modules:
  0.0 560.8 jit_solution(7697988557552064644)
XLA Ops:
  0.7 10.1 %copy.60 = f32[16,16,32,256]{3,0,2,1:T(8,128)S(1)} copy(f32[16,16,32,256]{3,2,1,0:T(8,128)} %param.7) | data formatting | bytes 16777216 | tf_op args[0]
  10.8 2.4 collective-permute-start.1
  13.3 1.8 collective-permute-start
  16.0 10.0 %constant_dynamic-update-slice_fusion.1 = f32[16,18,32,256]{3,0,2,1:T(8,128)} fusion(f32[16,18,32,256]{3,0,2,1:T(8,128)} %constant_dynamic-update-slice_fusion.2, f32[16,16,32,256]{3,2,1,0:T(8,128)S(1)} %copy-done), kind=kLoop, calls=%fused_computation.202 | loop fusion | bytes 16777216
  29.3 4.9 collective-permute-start.3
  34.9 2.1 multiply_add_fusion
  38.4 25.3 %fusion.81 = f32[16,16,32,256]{3,0,2,1:T(8,128)} fusion(f32[16,16,32,256]{3,0,2,1:T(8,128)} %copy-done.2, f32[16,18,32,256]{3,0,2,1:T(8,128)} %constant_dynamic-update-slice_fusion, f32[16,18,1,256]{3,0,2,1:T(8,128)S(1)} %collective-permute-done.3, f32[16,18,1,256]{3,0,2,1:T(8,128)S(1)} %collective-permute-done.2, ...), kind=kLoop, calls=%fused_computation.158 | loop fusion | flops 41943040 | bytes 29032460 | tf_op jit(solution)/shard_map/jit(_where)/select_n | solution.py:42
  66.3 7.8 %collective-permute-start.5 = (f32[16,1,32,256]{3,0,2,1:T(8,128)S(1)}, f32[16,1,32,256]{3,0,2,1:T(8,128)S(1)}, u32[]{:S(2)}, u32[]{:S(2)}) collective-permute-start(f32[16,1,32,256]{3,0,2,1:T(8,128)S(1)} %get-tuple-element.40), channel_id=1, source_target_pairs={{0,4},{4,8},{8,12},{12,16},{16,20},{20,24},{24,28},{1,5},{5,9},{9,... | collective-permute-start | bytes 1572872 | tf_op jit(solution)/shard_map/ppermute | solution.py:19
  74.1 1.5 collective-permute-done.5
  78.0 4.9 collective-permute-start.7
  82.9 2.6 collective-permute-done.6
  85.5 1.5 collective-permute-done.7
  86.9 24.8 %fusion.87 = f32[16,16,32,256]{3,0,2,1:T(8,128)} fusion(f32[16,16,32,256]{3,0,2,1:T(8,128)} %fusion.81, f32[16,1,32,256]{3,0,2,1:T(8,128)S(1)} %collective-permute-done.4, f32[16,1,32,256]{3,0,2,1:T(8,128)S(1)} %collective-permute-done.5, f32[16,18,1,256]{3,0,2,1:T(8,128)S(1)} %collective-permute-done.7, f32[16,18,1,256]{3,0,2,1:T(8,128)S(1)} %collective-permute-done.6, ...), kind=kLoop, calls=%fused_computation.164 | loop fusion | flops 50331648 | bytes 27983884 | tf_op jit(solution)/shard_map/jit(_where)/select_n | solution.py:42
  114.4 12.9 %collective-permute-start.9 = (f32[16,1,32,256]{3,0,2,1:T(8,128)S(1)}, f32[16,1,32,256]{3,0,2,1:T(8,128)S(1)}, u32[]{:S(2)}, u32[]{:S(2)}) collective-permute-start(f32[16,1,32,256]{3,0,2,1:T(8,128)S(1)} %get-tuple-element.38), channel_id=1, source_target_pairs={{0,4},{4,8},{8,12},{12,16},{16,20},{20,24},{24,28},{1,5},{5,9},{9,... | collective-permute-start | bytes 1572872 | tf_op jit(solution)/shard_map/ppermute | solution.py:19
  127.3 1.5 collective-permute-done.9
  131.2 4.7 collective-permute-start.11
  135.9 2.7 collective-permute-done.10
  140.1 24.8 %fusion.86 = f32[16,16,32,256]{3,0,2,1:T(8,128)} fusion(f32[16,16,32,256]{3,0,2,1:T(8,128)} %fusion.87, f32[16,1,32,256]{3,0,2,1:T(8,128)S(1)} %collective-permute-done.8, f32[16,1,32,256]{3,0,2,1:T(8,128)S(1)} %collective-permute-done.9, f32[16,18,1,256]{3,0,2,1:T(8,128)S(1)} %collective-permute-done.11, ...), kind=kLoop, calls=%fused_computation.163 | loop fusion | flops 50331648 | bytes 27983884 | tf_op jit(solution)/shard_map/jit(_where)/select_n | solution.py:42
  167.4 10.1 %collective-permute-start.13 = (f32[16,1,32,256]{3,0,2,1:T(8,128)S(1)}, f32[16,1,32,256]{3,0,2,1:T(8,128)S(1)}, u32[]{:S(2)}, u32[]{:S(2)}) collective-permute-start(f32[16,1,32,256]{3,0,2,1:T(8,128)S(1)} %get-tuple-element.36), channel_id=1, source_target_pairs={{0,4},{4,8},{8,12},{12,16},{16,20},{20,24},{24,28},{1,5},{5,9},{9,... | collective-permute-start | bytes 1572872 | tf_op jit(solution)/shard_map/ppermute | solution.py:19
  177.6 1.5 collective-permute-done.13
  181.4 4.8 collective-permute-start.15
  186.3 2.7 collective-permute-done.14
  189.0 1.5 collective-permute-done.15
  190.5 24.2 %fusion.85 = f32[16,16,32,256]{3,0,2,1:T(8,128)S(1)} fusion(f32[16,16,32,256]{3,0,2,1:T(8,128)} %fusion.86, f32[16,1,32,256]{3,0,2,1:T(8,128)S(1)} %collective-permute-done.12, f32[16,1,32,256]{3,0,2,1:T(8,128)S(1)} %collective-permute-done.13, f32[16,18,1,256]{3,0,2,1:T(8,128)S(1)} %collective-permute-done.15, ...), kind=kLoop, calls=%fused_computation.162 | loop fusion | flops 50331648 | bytes 27983884 | tf_op jit(solution)/shard_map/jit(_where)/select_n | solution.py:42
  216.1 9.8 %collective-permute-start.17 = (f32[16,1,32,256]{3,0,2,1:T(8,128)S(1)}, f32[16,1,32,256]{3,0,2,1:T(8,128)S(1)}, u32[]{:S(2)}, u32[]{:S(2)}) collective-permute-start(f32[16,1,32,256]{3,0,2,1:T(8,128)S(1)} %get-tuple-element.34), channel_id=1, source_target_pairs={{0,4},{4,8},{8,12},{12,16},{16,20},{20,24},{24,28},{1,5},{5,9},{9,... | collective-permute-start | bytes 1572872 | tf_op jit(solution)/shard_map/ppermute | solution.py:19
  225.9 1.5 collective-permute-done.17
  228.7 5.1 collective-permute-start.19
  233.8 2.5 collective-permute-done.18
  237.8 13.1 %fusion.80 = f32[16,16,32,256]{3,0,2,1:T(8,128)} fusion(f32[16,16,32,256]{3,0,2,1:T(8,128)S(1)} %fusion.85, f32[16,1,32,256]{3,0,2,1:T(8,128)S(1)} %collective-permute-done.16, f32[16,1,32,256]{3,0,2,1:T(8,128)S(1)} %collective-permute-done.17, f32[16,18,1,256]{3,0,2,1:T(8,128)S(1)} %collective-permute-done.19, ...), kind=kLoop, calls=%fused_computation.157 | loop fusion | flops 50331648 | bytes 19595276 | tf_op jit(solution)/shard_map/jit(_where)/select_n | solution.py:42
  253.5 9.8 %collective-permute-start.21 = (f32[16,1,32,256]{3,0,2,1:T(8,128)S(1)}, f32[16,1,32,256]{3,0,2,1:T(8,128)S(1)}, u32[]{:S(2)}, u32[]{:S(2)}) collective-permute-start(f32[16,1,32,256]{3,0,2,1:T(8,128)S(1)} %get-tuple-element.32), channel_id=1, source_target_pairs={{0,4},{4,8},{8,12},{12,16},{16,20},{20,24},{24,28},{1,5},{5,9},{9,... | collective-permute-start | bytes 1572872 | tf_op jit(solution)/shard_map/ppermute | solution.py:19
  263.3 1.5 collective-permute-done.21
  267.1 4.8 collective-permute-start.23
  272.0 2.7 collective-permute-done.22
  276.2 22.7 %fusion.84 = f32[16,16,32,256]{3,0,2,1:T(8,128)} fusion(f32[16,16,32,256]{3,0,2,1:T(8,128)S(1)} %fusion.85, f32[16,16,32,256]{3,0,2,1:T(8,128)} %fusion.80, f32[16,1,32,256]{3,0,2,1:T(8,128)S(1)} %collective-permute-done.20, f32[16,1,32,256]{3,0,2,1:T(8,128)S(1)} %collective-permute-done.21, f32[16,18,1,256]{3,0,2,1:T(8,128)S(1)} %collective-permute-done.23, ...), kind=kLoop, calls=%fused_computation.161 | loop fusion | flops 50331648 | bytes 27983884 | tf_op jit(solution)/shard_map/jit(_where)/select_n | solution.py:42
  301.5 11.3 %collective-permute-start.25 = (f32[16,1,32,256]{3,0,2,1:T(8,128)S(1)}, f32[16,1,32,256]{3,0,2,1:T(8,128)S(1)}, u32[]{:S(2)}, u32[]{:S(2)}) collective-permute-start(f32[16,1,32,256]{3,0,2,1:T(8,128)S(1)} %get-tuple-element.30), channel_id=1, source_target_pairs={{0,4},{4,8},{8,12},{12,16},{16,20},{20,24},{24,28},{1,5},{5,9},{9,... | collective-permute-start | bytes 1572872 | tf_op jit(solution)/shard_map/ppermute | solution.py:19
  312.8 1.5 collective-permute-done.25
  316.7 4.7 collective-permute-start.27
  322.1 2.1 collective-permute-done.26
  325.6 22.7 %fusion.83 = f32[16,16,32,256]{3,0,2,1:T(8,128)} fusion(f32[16,16,32,256]{3,0,2,1:T(8,128)S(1)} %fusion.85, f32[16,16,32,256]{3,0,2,1:T(8,128)} %fusion.84, f32[16,1,32,256]{3,0,2,1:T(8,128)S(1)} %collective-permute-done.24, f32[16,1,32,256]{3,0,2,1:T(8,128)S(1)} %collective-permute-done.25, f32[16,18,1,256]{3,0,2,1:T(8,128)S(1)} %collective-permute-done.27, ...), kind=kLoop, calls=%fused_computation.160 | loop fusion | flops 50331648 | bytes 27983884 | tf_op jit(solution)/shard_map/jit(_where)/select_n | solution.py:42
  350.9 13.9 %collective-permute-start.29 = (f32[16,1,32,256]{3,0,2,1:T(8,128)S(1)}, f32[16,1,32,256]{3,0,2,1:T(8,128)S(1)}, u32[]{:S(2)}, u32[]{:S(2)}) collective-permute-start(f32[16,1,32,256]{3,0,2,1:T(8,128)S(1)} %get-tuple-element.28), channel_id=1, source_target_pairs={{0,4},{4,8},{8,12},{12,16},{16,20},{20,24},{24,28},{1,5},{5,9},{9,... | collective-permute-start | bytes 1572872 | tf_op jit(solution)/shard_map/ppermute | solution.py:19
  368.7 4.7 collective-permute-start.31
  373.5 2.7 collective-permute-done.30
  377.7 22.7 %fusion.82 = f32[16,16,32,256]{3,0,2,1:T(8,128)} fusion(f32[16,16,32,256]{3,0,2,1:T(8,128)S(1)} %fusion.85, f32[16,16,32,256]{3,0,2,1:T(8,128)} %fusion.83, f32[16,1,32,256]{3,0,2,1:T(8,128)S(1)} %collective-permute-done.28, f32[16,1,32,256]{3,0,2,1:T(8,128)S(1)} %collective-permute-done.29, f32[16,18,1,256]{3,0,2,1:T(8,128)S(1)} %collective-permute-done.31, ...), kind=kLoop, calls=%fused_computation.159 | loop fusion | flops 50331648 | bytes 27983884 | tf_op jit(solution)/shard_map/jit(_where)/select_n | solution.py:42
  400.4 32.9 %copy.61 = f32[16,16,32,256]{0,3,2,1:T(8,128)} copy(f32[16,16,32,256]{3,0,2,1:T(8,128)} %fusion.82) | data formatting | bytes 16777216 | tf_op jit(solution)/shard_map/jit(_where)/select_n | solution.py:42
  433.3 1.8 gather_fusion
  436.0 39.7 %all-to-all-start = ((f32[32,1,128]{2,1,0:T(1,128)}), f32[32,1,128]{2,1,0:T(1,128)S(1)}, u32[]{:S(2)}, u32[]{:S(2)}) async-start(f32[32,1,128]{2,1,0:T(1,128)} %reshape.94), calls=%async_computation | async-start | bytes 32768 | tf_op jit(solution)/shard_map/all_to_all | solution.py:74
  475.7 11.6 %copy.66 = f32[16,16,32,256]{3,2,1,0:T(8,128)} copy(f32[16,16,32,256]{3,0,2,1:T(8,128)} %fusion.82) | data formatting | bytes 16777216
  489.2 70.7 %all-gather = f32[512,16]{1,0:T(8,128)S(1)} all-gather(f32[16,16]{1,0:T(8,128)S(1)} %fusion.109), channel_id=2, replica_groups=mesh['gx'=8,'gy'=4] {'gx','gy'}, dimensions={0}, use_global_device_ids=true | all-gather | bytes 33792 | tf_op jit(solution)/shard_map/all_gather | solution.py:82
  (85 shorter events, 50.7 us)
Async XLA Ops:
  0.6 15.4 %copy-start = (f32[16,16,32,256]{3,2,1,0:T(8,128)S(1)}, f32[16,16,32,256]{3,2,1,0:T(8,128)}, u32[]{:S(2)}) copy-start(f32[16,16,32,256]{3,2,1,0:T(8,128)} %param.7) | copy-start | bytes 25165828
  0.6 14.4 %copy-start.1 = (f32[16,32,256]{2,1,0:T(8,128)S(1)}, f32[16,32,256]{2,1,0:T(8,128)}, u32[]{:S(2)}) copy-start(f32[16,32,256]{2,1,0:T(8,128)} %param.8) | copy-start | bytes 1572868
  10.7 15.3 %copy-start.2 = (f32[16,16,32,256]{3,0,2,1:T(8,128)}, f32[16,16,32,256]{3,0,2,1:T(8,128)S(1)}, u32[]{:S(2)}) copy-start(f32[16,16,32,256]{3,0,2,1:T(8,128)S(1)} %copy.60) | copy-start | bytes 25165828
  10.8 4.4 collective-permute-start.1
  13.3 12.8 %collective-permute-start = (f32[16,1,32,256]{3,0,2,1:T(8,128)S(1)}, f32[16,1,32,256]{3,0,2,1:T(8,128)S(1)}, u32[]{:S(2)}, u32[]{:S(2)}) collective-permute-start(f32[16,1,32,256]{3,0,2,1:T(8,128)S(1)} %get-tuple-element.42), channel_id=1, source_target_pairs={{4,0},{8,4},{12,8},{16,12},{20,16},{24,20},{28,24},{5,1},{9,5},{13... | collective-permute-start | bytes 1572872 | tf_op jit(solution)/shard_map/ppermute | solution.py:21
  16.0 18.2 %copy-start.5 = (f32[3]{0:T(128)S(1)}, f32[3]{0:T(128)}, u32[]{:S(2)}) copy-start(f32[3]{0:T(128)} %param.9) | copy-start | bytes 40
  28.0 9.0 %collective-permute-start.2 = (f32[16,18,1,256]{3,0,2,1:T(8,128)S(1)}, f32[16,18,1,256]{3,0,2,1:T(8,128)S(1)}, u32[]{:S(2)}, u32[]{:S(2)}) collective-permute-start(f32[16,18,1,256]{3,0,2,1:T(8,128)S(1)} %get-tuple-element.26), channel_id=1, source_target_pairs={{1,0},{2,1},{3,2},{5,4},{6,5},{7,6},{9,8},{10,9},{11,10},{13,12},{... | collective-permute-start | bytes 884744 | tf_op jit(solution)/shard_map/ppermute | solution.py:21
  29.3 9.2 %collective-permute-start.3 = (f32[16,18,1,256]{3,0,2,1:T(8,128)S(1)}, f32[16,18,1,256]{3,0,2,1:T(8,128)S(1)}, u32[]{:S(2)}, u32[]{:S(2)}) collective-permute-start(f32[16,18,1,256]{3,0,2,1:T(8,128)S(1)} %get-tuple-element.27), channel_id=1, source_target_pairs={{0,1},{1,2},{2,3},{4,5},{5,6},{6,7},{8,9},{9,10},{10,11},{12,13},{... | collective-permute-start | bytes 884744 | tf_op jit(solution)/shard_map/ppermute | solution.py:19
  65.0 9.1 %collective-permute-start.4 = (f32[16,1,32,256]{3,0,2,1:T(8,128)S(1)}, f32[16,1,32,256]{3,0,2,1:T(8,128)S(1)}, u32[]{:S(2)}, u32[]{:S(2)}) collective-permute-start(f32[16,1,32,256]{3,0,2,1:T(8,128)S(1)} %get-tuple-element.41), channel_id=1, source_target_pairs={{4,0},{8,4},{12,8},{16,12},{20,16},{24,20},{28,24},{5,1},{9,5},{13... | collective-permute-start | bytes 1572872 | tf_op jit(solution)/shard_map/ppermute | solution.py:21
  66.3 9.3 %collective-permute-start.5 = (f32[16,1,32,256]{3,0,2,1:T(8,128)S(1)}, f32[16,1,32,256]{3,0,2,1:T(8,128)S(1)}, u32[]{:S(2)}, u32[]{:S(2)}) collective-permute-start(f32[16,1,32,256]{3,0,2,1:T(8,128)S(1)} %get-tuple-element.40), channel_id=1, source_target_pairs={{0,4},{4,8},{8,12},{12,16},{16,20},{20,24},{24,28},{1,5},{5,9},{9,... | collective-permute-start | bytes 1572872 | tf_op jit(solution)/shard_map/ppermute | solution.py:19
  76.7 8.8 %collective-permute-start.6 = (f32[16,18,1,256]{3,0,2,1:T(8,128)S(1)}, f32[16,18,1,256]{3,0,2,1:T(8,128)S(1)}, u32[]{:S(2)}, u32[]{:S(2)}) collective-permute-start(f32[16,18,1,256]{3,0,2,1:T(8,128)S(1)} %get-tuple-element.24), channel_id=1, source_target_pairs={{1,0},{2,1},{3,2},{5,4},{6,5},{7,6},{9,8},{10,9},{11,10},{13,12},{... | collective-permute-start | bytes 884744 | tf_op jit(solution)/shard_map/ppermute | solution.py:21
  78.0 8.9 %collective-permute-start.7 = (f32[16,18,1,256]{3,0,2,1:T(8,128)S(1)}, f32[16,18,1,256]{3,0,2,1:T(8,128)S(1)}, u32[]{:S(2)}, u32[]{:S(2)}) collective-permute-start(f32[16,18,1,256]{3,0,2,1:T(8,128)S(1)} %get-tuple-element.25), channel_id=1, source_target_pairs={{0,1},{1,2},{2,3},{4,5},{5,6},{6,7},{8,9},{9,10},{10,11},{12,13},{... | collective-permute-start | bytes 884744 | tf_op jit(solution)/shard_map/ppermute | solution.py:19
  113.1 14.2 %collective-permute-start.8 = (f32[16,1,32,256]{3,0,2,1:T(8,128)S(1)}, f32[16,1,32,256]{3,0,2,1:T(8,128)S(1)}, u32[]{:S(2)}, u32[]{:S(2)}) collective-permute-start(f32[16,1,32,256]{3,0,2,1:T(8,128)S(1)} %get-tuple-element.39), channel_id=1, source_target_pairs={{4,0},{8,4},{12,8},{16,12},{20,16},{24,20},{28,24},{5,1},{9,5},{13... | collective-permute-start | bytes 1572872 | tf_op jit(solution)/shard_map/ppermute | solution.py:21
  114.4 14.4 %collective-permute-start.9 = (f32[16,1,32,256]{3,0,2,1:T(8,128)S(1)}, f32[16,1,32,256]{3,0,2,1:T(8,128)S(1)}, u32[]{:S(2)}, u32[]{:S(2)}) collective-permute-start(f32[16,1,32,256]{3,0,2,1:T(8,128)S(1)} %get-tuple-element.38), channel_id=1, source_target_pairs={{0,4},{4,8},{8,12},{12,16},{16,20},{20,24},{24,28},{1,5},{5,9},{9,... | collective-permute-start | bytes 1572872 | tf_op jit(solution)/shard_map/ppermute | solution.py:19
  129.9 8.8 %collective-permute-start.10 = (f32[16,18,1,256]{3,0,2,1:T(8,128)S(1)}, f32[16,18,1,256]{3,0,2,1:T(8,128)S(1)}, u32[]{:S(2)}, u32[]{:S(2)}) collective-permute-start(f32[16,18,1,256]{3,0,2,1:T(8,128)S(1)} %get-tuple-element.22), channel_id=1, source_target_pairs={{1,0},{2,1},{3,2},{5,4},{6,5},{7,6},{9,8},{10,9},{11,10},{13,12},{... | collective-permute-start | bytes 884744 | tf_op jit(solution)/shard_map/ppermute | solution.py:21
  131.2 8.9 %collective-permute-start.11 = (f32[16,18,1,256]{3,0,2,1:T(8,128)S(1)}, f32[16,18,1,256]{3,0,2,1:T(8,128)S(1)}, u32[]{:S(2)}, u32[]{:S(2)}) collective-permute-start(f32[16,18,1,256]{3,0,2,1:T(8,128)S(1)} %get-tuple-element.23), channel_id=1, source_target_pairs={{0,1},{1,2},{2,3},{4,5},{5,6},{6,7},{8,9},{9,10},{10,11},{12,13},{... | collective-permute-start | bytes 884744 | tf_op jit(solution)/shard_map/ppermute | solution.py:19
  166.1 11.4 %collective-permute-start.12 = (f32[16,1,32,256]{3,0,2,1:T(8,128)S(1)}, f32[16,1,32,256]{3,0,2,1:T(8,128)S(1)}, u32[]{:S(2)}, u32[]{:S(2)}) collective-permute-start(f32[16,1,32,256]{3,0,2,1:T(8,128)S(1)} %get-tuple-element.37), channel_id=1, source_target_pairs={{4,0},{8,4},{12,8},{16,12},{20,16},{24,20},{28,24},{5,1},{9,5},{13... | collective-permute-start | bytes 1572872 | tf_op jit(solution)/shard_map/ppermute | solution.py:21
  167.4 11.6 %collective-permute-start.13 = (f32[16,1,32,256]{3,0,2,1:T(8,128)S(1)}, f32[16,1,32,256]{3,0,2,1:T(8,128)S(1)}, u32[]{:S(2)}, u32[]{:S(2)}) collective-permute-start(f32[16,1,32,256]{3,0,2,1:T(8,128)S(1)} %get-tuple-element.36), channel_id=1, source_target_pairs={{0,4},{4,8},{8,12},{12,16},{16,20},{20,24},{24,28},{1,5},{5,9},{9,... | collective-permute-start | bytes 1572872 | tf_op jit(solution)/shard_map/ppermute | solution.py:19
  180.1 8.9 %collective-permute-start.14 = (f32[16,18,1,256]{3,0,2,1:T(8,128)S(1)}, f32[16,18,1,256]{3,0,2,1:T(8,128)S(1)}, u32[]{:S(2)}, u32[]{:S(2)}) collective-permute-start(f32[16,18,1,256]{3,0,2,1:T(8,128)S(1)} %get-tuple-element.20), channel_id=1, source_target_pairs={{1,0},{2,1},{3,2},{5,4},{6,5},{7,6},{9,8},{10,9},{11,10},{13,12},{... | collective-permute-start | bytes 884744 | tf_op jit(solution)/shard_map/ppermute | solution.py:21
  181.4 9.1 %collective-permute-start.15 = (f32[16,18,1,256]{3,0,2,1:T(8,128)S(1)}, f32[16,18,1,256]{3,0,2,1:T(8,128)S(1)}, u32[]{:S(2)}, u32[]{:S(2)}) collective-permute-start(f32[16,18,1,256]{3,0,2,1:T(8,128)S(1)} %get-tuple-element.21), channel_id=1, source_target_pairs={{0,1},{1,2},{2,3},{4,5},{5,6},{6,7},{8,9},{9,10},{10,11},{12,13},{... | collective-permute-start | bytes 884744 | tf_op jit(solution)/shard_map/ppermute | solution.py:19
  214.8 11.1 %collective-permute-start.16 = (f32[16,1,32,256]{3,0,2,1:T(8,128)S(1)}, f32[16,1,32,256]{3,0,2,1:T(8,128)S(1)}, u32[]{:S(2)}, u32[]{:S(2)}) collective-permute-start(f32[16,1,32,256]{3,0,2,1:T(8,128)S(1)} %get-tuple-element.35), channel_id=1, source_target_pairs={{4,0},{8,4},{12,8},{16,12},{20,16},{24,20},{28,24},{5,1},{9,5},{13... | collective-permute-start | bytes 1572872 | tf_op jit(solution)/shard_map/ppermute | solution.py:21
  216.1 11.3 %collective-permute-start.17 = (f32[16,1,32,256]{3,0,2,1:T(8,128)S(1)}, f32[16,1,32,256]{3,0,2,1:T(8,128)S(1)}, u32[]{:S(2)}, u32[]{:S(2)}) collective-permute-start(f32[16,1,32,256]{3,0,2,1:T(8,128)S(1)} %get-tuple-element.34), channel_id=1, source_target_pairs={{0,4},{4,8},{8,12},{12,16},{16,20},{20,24},{24,28},{1,5},{5,9},{9,... | collective-permute-start | bytes 1572872 | tf_op jit(solution)/shard_map/ppermute | solution.py:19
  227.4 8.9 %collective-permute-start.18 = (f32[16,18,1,256]{3,0,2,1:T(8,128)S(1)}, f32[16,18,1,256]{3,0,2,1:T(8,128)S(1)}, u32[]{:S(2)}, u32[]{:S(2)}) collective-permute-start(f32[16,18,1,256]{3,0,2,1:T(8,128)S(1)} %get-tuple-element.18), channel_id=1, source_target_pairs={{1,0},{2,1},{3,2},{5,4},{6,5},{7,6},{9,8},{10,9},{11,10},{13,12},{... | collective-permute-start | bytes 884744 | tf_op jit(solution)/shard_map/ppermute | solution.py:21
  228.7 9.1 %collective-permute-start.19 = (f32[16,18,1,256]{3,0,2,1:T(8,128)S(1)}, f32[16,18,1,256]{3,0,2,1:T(8,128)S(1)}, u32[]{:S(2)}, u32[]{:S(2)}) collective-permute-start(f32[16,18,1,256]{3,0,2,1:T(8,128)S(1)} %get-tuple-element.19), channel_id=1, source_target_pairs={{0,1},{1,2},{2,3},{4,5},{5,6},{6,7},{8,9},{9,10},{10,11},{12,13},{... | collective-permute-start | bytes 884744 | tf_op jit(solution)/shard_map/ppermute | solution.py:19
  252.2 11.1 %collective-permute-start.20 = (f32[16,1,32,256]{3,0,2,1:T(8,128)S(1)}, f32[16,1,32,256]{3,0,2,1:T(8,128)S(1)}, u32[]{:S(2)}, u32[]{:S(2)}) collective-permute-start(f32[16,1,32,256]{3,0,2,1:T(8,128)S(1)} %get-tuple-element.33), channel_id=1, source_target_pairs={{4,0},{8,4},{12,8},{16,12},{20,16},{24,20},{28,24},{5,1},{9,5},{13... | collective-permute-start | bytes 1572872 | tf_op jit(solution)/shard_map/ppermute | solution.py:21
  253.5 11.3 %collective-permute-start.21 = (f32[16,1,32,256]{3,0,2,1:T(8,128)S(1)}, f32[16,1,32,256]{3,0,2,1:T(8,128)S(1)}, u32[]{:S(2)}, u32[]{:S(2)}) collective-permute-start(f32[16,1,32,256]{3,0,2,1:T(8,128)S(1)} %get-tuple-element.32), channel_id=1, source_target_pairs={{0,4},{4,8},{8,12},{12,16},{16,20},{20,24},{24,28},{1,5},{5,9},{9,... | collective-permute-start | bytes 1572872 | tf_op jit(solution)/shard_map/ppermute | solution.py:19
  265.8 8.9 %collective-permute-start.22 = (f32[16,18,1,256]{3,0,2,1:T(8,128)S(1)}, f32[16,18,1,256]{3,0,2,1:T(8,128)S(1)}, u32[]{:S(2)}, u32[]{:S(2)}) collective-permute-start(f32[16,18,1,256]{3,0,2,1:T(8,128)S(1)} %get-tuple-element.16), channel_id=1, source_target_pairs={{1,0},{2,1},{3,2},{5,4},{6,5},{7,6},{9,8},{10,9},{11,10},{13,12},{... | collective-permute-start | bytes 884744 | tf_op jit(solution)/shard_map/ppermute | solution.py:21
  267.1 9.1 %collective-permute-start.23 = (f32[16,18,1,256]{3,0,2,1:T(8,128)S(1)}, f32[16,18,1,256]{3,0,2,1:T(8,128)S(1)}, u32[]{:S(2)}, u32[]{:S(2)}) collective-permute-start(f32[16,18,1,256]{3,0,2,1:T(8,128)S(1)} %get-tuple-element.17), channel_id=1, source_target_pairs={{0,1},{1,2},{2,3},{4,5},{5,6},{6,7},{8,9},{9,10},{10,11},{12,13},{... | collective-permute-start | bytes 884744 | tf_op jit(solution)/shard_map/ppermute | solution.py:19
  300.2 12.6 %collective-permute-start.24 = (f32[16,1,32,256]{3,0,2,1:T(8,128)S(1)}, f32[16,1,32,256]{3,0,2,1:T(8,128)S(1)}, u32[]{:S(2)}, u32[]{:S(2)}) collective-permute-start(f32[16,1,32,256]{3,0,2,1:T(8,128)S(1)} %get-tuple-element.31), channel_id=1, source_target_pairs={{4,0},{8,4},{12,8},{16,12},{20,16},{24,20},{28,24},{5,1},{9,5},{13... | collective-permute-start | bytes 1572872 | tf_op jit(solution)/shard_map/ppermute | solution.py:21
  301.5 12.8 %collective-permute-start.25 = (f32[16,1,32,256]{3,0,2,1:T(8,128)S(1)}, f32[16,1,32,256]{3,0,2,1:T(8,128)S(1)}, u32[]{:S(2)}, u32[]{:S(2)}) collective-permute-start(f32[16,1,32,256]{3,0,2,1:T(8,128)S(1)} %get-tuple-element.30), channel_id=1, source_target_pairs={{0,4},{4,8},{8,12},{12,16},{16,20},{20,24},{24,28},{1,5},{5,9},{9,... | collective-permute-start | bytes 1572872 | tf_op jit(solution)/shard_map/ppermute | solution.py:19
  315.4 8.8 %collective-permute-start.26 = (f32[16,18,1,256]{3,0,2,1:T(8,128)S(1)}, f32[16,18,1,256]{3,0,2,1:T(8,128)S(1)}, u32[]{:S(2)}, u32[]{:S(2)}) collective-permute-start(f32[16,18,1,256]{3,0,2,1:T(8,128)S(1)} %get-tuple-element.14), channel_id=1, source_target_pairs={{1,0},{2,1},{3,2},{5,4},{6,5},{7,6},{9,8},{10,9},{11,10},{13,12},{... | collective-permute-start | bytes 884744 | tf_op jit(solution)/shard_map/ppermute | solution.py:21
  316.7 8.9 %collective-permute-start.27 = (f32[16,18,1,256]{3,0,2,1:T(8,128)S(1)}, f32[16,18,1,256]{3,0,2,1:T(8,128)S(1)}, u32[]{:S(2)}, u32[]{:S(2)}) collective-permute-start(f32[16,18,1,256]{3,0,2,1:T(8,128)S(1)} %get-tuple-element.15), channel_id=1, source_target_pairs={{0,1},{1,2},{2,3},{4,5},{5,6},{6,7},{8,9},{9,10},{10,11},{12,13},{... | collective-permute-start | bytes 884744 | tf_op jit(solution)/shard_map/ppermute | solution.py:19
  322.1 42.8 %copy-start.7 = (s32[1,1,128,1]{2,3,1,0:T(1,128)S(1)}, s32[1,1,128,1]{2,3,1,0:T(1,128)}, u32[]{:S(2)}) copy-start(s32[1,1,128,1]{2,3,1,0:T(1,128)} %param.11) | copy-start | bytes 1540
  322.1 43.0 %copy-start.6 = (s32[1,1,128]{2,1,0:T(1,128)S(1)}, s32[1,1,128]{2,1,0:T(1,128)}, u32[]{:S(2)}) copy-start(s32[1,1,128]{2,1,0:T(1,128)} %param.10) | copy-start | bytes 1540
  349.6 15.5 %collective-permute-start.28 = (f32[16,1,32,256]{3,0,2,1:T(8,128)S(1)}, f32[16,1,32,256]{3,0,2,1:T(8,128)S(1)}, u32[]{:S(2)}, u32[]{:S(2)}) collective-permute-start(f32[16,1,32,256]{3,0,2,1:T(8,128)S(1)} %get-tuple-element.29), channel_id=1, source_target_pairs={{4,0},{8,4},{12,8},{16,12},{20,16},{24,20},{28,24},{5,1},{9,5},{13... | collective-permute-start | bytes 1572872 | tf_op jit(solution)/shard_map/ppermute | solution.py:21
  350.9 15.4 %collective-permute-start.29 = (f32[16,1,32,256]{3,0,2,1:T(8,128)S(1)}, f32[16,1,32,256]{3,0,2,1:T(8,128)S(1)}, u32[]{:S(2)}, u32[]{:S(2)}) collective-permute-start(f32[16,1,32,256]{3,0,2,1:T(8,128)S(1)} %get-tuple-element.28), channel_id=1, source_target_pairs={{0,4},{4,8},{8,12},{12,16},{16,20},{20,24},{24,28},{1,5},{5,9},{9,... | collective-permute-start | bytes 1572872 | tf_op jit(solution)/shard_map/ppermute | solution.py:19
  367.4 8.8 %collective-permute-start.30 = (f32[16,18,1,256]{3,0,2,1:T(8,128)S(1)}, f32[16,18,1,256]{3,0,2,1:T(8,128)S(1)}, u32[]{:S(2)}, u32[]{:S(2)}) collective-permute-start(f32[16,18,1,256]{3,0,2,1:T(8,128)S(1)} %get-tuple-element.12), channel_id=1, source_target_pairs={{1,0},{2,1},{3,2},{5,4},{6,5},{7,6},{9,8},{10,9},{11,10},{13,12},{... | collective-permute-start | bytes 884744 | tf_op jit(solution)/shard_map/ppermute | solution.py:21
  368.7 8.9 %collective-permute-start.31 = (f32[16,18,1,256]{3,0,2,1:T(8,128)S(1)}, f32[16,18,1,256]{3,0,2,1:T(8,128)S(1)}, u32[]{:S(2)}, u32[]{:S(2)}) collective-permute-start(f32[16,18,1,256]{3,0,2,1:T(8,128)S(1)} %get-tuple-element.13), channel_id=1, source_target_pairs={{0,1},{1,2},{2,3},{4,5},{5,6},{6,7},{8,9},{9,10},{10,11},{12,13},{... | collective-permute-start | bytes 884744 | tf_op jit(solution)/shard_map/ppermute | solution.py:19
  400.4 34.7 %copy-start.4 = (f32[1,1,128,16]{2,3,1,0:T(8,128)S(1)}, f32[1,1,128,16]{2,3,1,0:T(8,128)}, u32[]{:S(2)}) copy-start(f32[1,1,128,16]{2,3,1,0:T(8,128)} %param.13) | copy-start | bytes 24580
  436.0 51.3 %all-to-all-start = ((f32[32,1,128]{2,1,0:T(1,128)}), f32[32,1,128]{2,1,0:T(1,128)S(1)}, u32[]{:S(2)}, u32[]{:S(2)}) async-start(f32[32,1,128]{2,1,0:T(1,128)} %reshape.94), calls=%async_computation | async-start | bytes 32768 | tf_op jit(solution)/shard_map/all_to_all | solution.py:74
  488.9 71.6 %copy-start.3 = (f32[16,16]{1,0:T(8,128)}, f32[16,16]{1,0:T(8,128)S(1)}, u32[]{:S(2)}) copy-start(f32[16,16]{1,0:T(8,128)S(1)} %convolution_bitcast_fusion) | copy-start | bytes 3076
